TPU v7x, 32 devices: a whole 2x2x4 slice. The times are simulated.
32 devices in a mesh: blk: 8 (over y, x, core), col: 4 (over z).
Axes of the slice: x: 2, y: 2, z: 4, core: 2. Of those that a mesh axis runs over, the one named last changes fastest.
Arguments:
- samples: bfloat16 [2048, 768], P('blk'), may hold values from -3 to 3
- targets: float32 [2048, 256], P('blk'), may hold values from -6 to 6
- batch_index: int32 [1024], P('blk'), may hold values from 0 to 255
- centers: bfloat16 [4096, 768], P(('blk', 'col')), may hold values from -3 to 3
- weights: float32 [4096, 256], P(('blk', 'col')), may hold values from -6 to 6
- nystrom_index: int32 [1536], replicated, may hold values from 0 to 4095, as said below
- eigvecs: float32 [1536, 128], replicated, may hold values from -0.15625 to 0.15625
- coefficient: float32 [128], replicated, may hold values from 0.4 to 0.95
Outputs:
- residual: float32 [1024, 256], P(('blk', 'col'))
- new_weights: float32 [4096, 256], P(('blk', 'col'))
Inputs may be any that keep to these rules, and one draw needn't show every extreme that they name: Batch row i is sample row (i // 128) * 256 + batch_index[i]. `nystrom_index`: 1536 distinct center rows.
All inputs are finite; a program needn't handle non-finite values.
Results may differ from a plain program's by a relative error of at most 0.0003.
The roundings to bfloat16 on the way count: a program that leaves them out, or rounds other values in their place, can miss the bound.
Values may be sent and summed in bfloat16 or wider, within the bound.
No kernel may reach another device: no remote copies, remote signals or barrier semaphores. Data moves between devices by JAX's collectives and lax.ppermute only.
A program may use at most 64 MiB of HBM per device.

v0:
```python
import jax
import jax.numpy as jnp
from jax import lax
from jax.sharding import PartitionSpec as P

spread = 1.0
shift_sq = 1.0
step_size = 4.0


def shifted(block, axis, distance):
    devices = range(lax.axis_size(axis))
    route = [((i - distance) % len(devices), i) for i in devices]
    return lax.ppermute(block, axis, route)


def kernel_block(points, centers, center_sq):
    point_sq = jnp.sum(jnp.square(points.astype(jnp.float32)), axis=1, keepdims=True)
    cross = lax.dot_general(
        points, centers, (((1,), (1,)), ((), ())), preferred_element_type=jnp.float32
    )
    dist_sq = point_sq + center_sq[None, :] - 2.0 * cross
    return jnp.exp(-jnp.sqrt(dist_sq + shift_sq) / spread).astype(jnp.bfloat16)


def move_up(points_now):
    return shifted(points_now, "blk", 1)


def pass_up(partial_value):
    return shifted(partial_value, "blk", 1)


def local(samples, targets, batch_index, centers, weights, nystrom_index, eigvecs, coefficient):
    blocks = lax.axis_size("blk")
    columns = lax.axis_size("col")
    my_block = lax.axis_index("blk")
    blk_rows = batch_index.shape[0]
    n_center = centers.shape[0]
    out_width = weights.shape[1]
    points = jnp.take(samples, batch_index, axis=0)
    wanted = jnp.take(targets, batch_index, axis=0)
    center_sq = jnp.sum(jnp.square(centers.astype(jnp.float32)), axis=1)
    weights_low = weights.astype(jnp.bfloat16)
    kernel_store = jnp.zeros((blocks * blk_rows, n_center), jnp.bfloat16)

    def absorb(points_now, partial_value, stored, offset):
        kernel = kernel_block(points_now, centers, center_sq)
        stored = lax.dynamic_update_slice(stored, kernel, (offset, 0))
        return (
            partial_value + jnp.dot(kernel, weights_low, preferred_element_type=jnp.float32),
            stored,
        )

    def walk_step(step_idx, state_now):
        points_now, partial_value, stored = state_now
        partial_value, stored = absorb(
            points_now, partial_value, stored, (my_block - step_idx) % blocks * blk_rows
        )
        return (move_up(points_now), pass_up(partial_value), stored)

    initial = (points, jnp.zeros((blk_rows, out_width), jnp.float32), kernel_store)
    points_now, partial_value, kernel_store = lax.fori_loop(0, blocks - 1, walk_step, initial)
    partial_value, kernel_store = absorb(
        points_now, partial_value, kernel_store, (my_block + 1) % blocks * blk_rows
    )
    partial_value = pass_up(partial_value)
    share_rows = blk_rows // columns
    prediction = lax.psum(partial_value, "col")
    residual_full = prediction - wanted
    gathered = lax.all_gather(residual_full.astype(jnp.bfloat16), "blk", axis=0, tiled=True)
    own_resid = lax.dynamic_slice_in_dim(
        residual_full, lax.axis_index("col") * share_rows, share_rows, 0
    )
    gradient = lax.dot_general(
        kernel_store, gathered, (((0,), (0,)), ((), ())), preferred_element_type=jnp.float32
    )
    first_row = lax.axis_index(("blk", "col")) * n_center
    position = nystrom_index - first_row
    inside = (position >= 0) & (position < n_center)
    position = jnp.where(inside, position, n_center)
    target_row = jnp.minimum(position, n_center - 1)
    picked = jnp.where(inside[:, None], jnp.take(gradient, target_row, axis=0), 0.0)
    highest = lax.Precision.HIGHEST
    local_proj = lax.dot_general(eigvecs, picked, (((0,), (0,)), ((), ())), precision=highest)
    projected = lax.psum(local_proj, ("blk", "col"))
    correction = jnp.dot(eigvecs, coefficient[:, None] * projected, precision=highest)
    adjusted = gradient.at[position].add(-correction, mode="drop")
    return (own_resid, weights - step_size * adjusted)


def solution(mesh):
    in_specs = (
        P("blk", None),
        P("blk", None),
        P("blk"),
        P(("blk", "col"), None),
        P(("blk", "col"), None),
        P(),
        P(),
        P(),
    )
    out_specs = (P(("blk", "col"), None), P(("blk", "col"), None))
    return jax.shard_map(local, mesh=mesh, in_specs=in_specs, out_specs=out_specs, check_vma=False)
```

profile of v0, /device:TPU:0, one launch (start us, length us, event | category | flops | bytes accessed | tf_op | source)
XLA Modules:
  0.0 271.0 jit_solution(4618817647422644272)
XLA Ops:
  7.2 0.8 compare_and_fusion.2
  8.0 0.7 compare_select_fusion.2
  8.7 1.0 multiply_reduce_fusion.2
  9.7 0.9 convert_element_type.36
  10.6 2.0 gather_fusion
  12.8 53.1 %while.19 = (s32[]{:T(128)}, bf16[128,768]{1,0:T(8,128)(2,1)S(1)}, f32[128,256]{1,0:T(8,128)S(1)}, bf16[1024,128]{1,0:T(8,128)(2,1)S(1)}, f32[128]{0:T(128)S(1)}...) while((s32[]{:T(128)}, bf16[128,768]{1,0:T(8,128)(2,1)S(1)}, ...), condition=%wide.region_3.4_spmd, body=%wide.region_1.3_spmd.sunk | while | flops 33980304 | bytes 2721664 | solution.py:63
  12.9 0.5 collective-permute-start
  14.0 2.6 collective-permute-start.1
  16.6 4.4 %collective-permute-done.1 = f32[128,256]{1,0:T(8,128)S(1)} collective-permute-done((f32[128,256]{1,0:T(8,128)S(1)}, f32[128,256]{1,0:T(8,128)S(1)}, u32[]{:S(2)}, u32[]{:S(2)}) %collective-permute-start.1) | collective-permute-done | bytes 131104 | tf_op jit(solution)/shard_map/while/body/eval_jaxpr/ppermute | solution.py:14
  21.7 1.5 collective-permute-start.1
  23.2 5.3 %collective-permute-done.1 = f32[128,256]{1,0:T(8,128)S(1)} collective-permute-done((f32[128,256]{1,0:T(8,128)S(1)}, f32[128,256]{1,0:T(8,128)S(1)}, u32[]{:S(2)}, u32[]{:S(2)}) %collective-permute-start.1) | collective-permute-done | bytes 131104 | tf_op jit(solution)/shard_map/while/body/eval_jaxpr/ppermute | solution.py:14
  29.2 0.6 collective-permute-start.1
  29.7 6.2 %collective-permute-done.1 = f32[128,256]{1,0:T(8,128)S(1)} collective-permute-done((f32[128,256]{1,0:T(8,128)S(1)}, f32[128,256]{1,0:T(8,128)S(1)}, u32[]{:S(2)}, u32[]{:S(2)}) %collective-permute-start.1) | collective-permute-done | bytes 131104 | tf_op jit(solution)/shard_map/while/body/eval_jaxpr/ppermute | solution.py:14
  36.7 6.8 %collective-permute-done.1 = f32[128,256]{1,0:T(8,128)S(1)} collective-permute-done((f32[128,256]{1,0:T(8,128)S(1)}, f32[128,256]{1,0:T(8,128)S(1)}, u32[]{:S(2)}, u32[]{:S(2)}) %collective-permute-start.1) | collective-permute-done | bytes 131104 | tf_op jit(solution)/shard_map/while/body/eval_jaxpr/ppermute | solution.py:14
  44.2 6.8 %collective-permute-done.1 = f32[128,256]{1,0:T(8,128)S(1)} collective-permute-done((f32[128,256]{1,0:T(8,128)S(1)}, f32[128,256]{1,0:T(8,128)S(1)}, u32[]{:S(2)}, u32[]{:S(2)}) %collective-permute-start.1) | collective-permute-done | bytes 131104 | tf_op jit(solution)/shard_map/while/body/eval_jaxpr/ppermute | solution.py:14
  51.7 6.8 %collective-permute-done.1 = f32[128,256]{1,0:T(8,128)S(1)} collective-permute-done((f32[128,256]{1,0:T(8,128)S(1)}, f32[128,256]{1,0:T(8,128)S(1)}, u32[]{:S(2)}, u32[]{:S(2)}) %collective-permute-start.1) | collective-permute-done | bytes 131104 | tf_op jit(solution)/shard_map/while/body/eval_jaxpr/ppermute | solution.py:14
  59.1 6.8 %collective-permute-done.1 = f32[128,256]{1,0:T(8,128)S(1)} collective-permute-done((f32[128,256]{1,0:T(8,128)S(1)}, f32[128,256]{1,0:T(8,128)S(1)}, u32[]{:S(2)}, u32[]{:S(2)}) %collective-permute-start.1) | collective-permute-done | bytes 131104 | tf_op jit(solution)/shard_map/while/body/eval_jaxpr/ppermute | solution.py:14
  66.5 5.2 %collective-permute-done.2 = f32[128,256]{1,0:T(8,128)S(1)} collective-permute-done((f32[128,256]{1,0:T(8,128)S(1)}, f32[128,256]{1,0:T(8,128)S(1)}, u32[]{:S(2)}, u32[]{:S(2)}) %collective-permute-start.2) | collective-permute-done | bytes 131104 | tf_op jit(solution)/shard_map/ppermute | solution.py:14
  71.8 0.7 copy-done.4
  72.5 0.8 gather_fusion.1
  73.3 35.0 %all-reduce.3.cloned.1.call-done = f32[128,256]{1,0:T(8,128)} async-done(((f32[128,256]{1,0:T(8,128)}), f32[128,256]{1,0:T(8,128)}) %all-reduce.3.cloned.1.call-update) | async-done | bytes 131088 | tf_op jit(solution)/shard_map/psum | solution.py:69
  108.3 1.0 fusion.27
  109.3 9.8 %all_gather.3 = bf16[1024,256]{1,0:T(8,128)(2,1)S(1)} all-gather(bf16[128,256]{1,0:T(8,128)(2,1)S(1)} %get-tuple-element.224), channel_id=1, replica_groups=mesh['blk'=8,'col'=4] {'blk'}, dimensions={0}, use_global_device_ids=true | all-gather | bytes 589824 | tf_op jit(solution)/shard_map/all_gather | solution.py:71
  119.1 0.3 fusion.28
  119.4 3.7 %gather_fusion.2 = f32[1536,256]{1,0:T(8,128)S(1)} fusion(f32[128,256]{1,0:T(8,128)S(1)} %fusion.28, s32[2048]{0:T(1024)S(1)} %pad_clamp_fusion), kind=kCustom, calls=%fused_computation.2 | custom fusion | bytes 3151872 | tf_op jit(solution)/shard_map/jit(_take)/gather | solution.py:83
  123.1 2.6 fusion.10
  125.7 0.6 constant_dynamic-slice_fusion
  126.3 122.8 %all-reduce.5.cloned.1.call-done = f32[128,256]{1,0:T(8,128)} async-done(((f32[128,256]{1,0:T(8,128)}), f32[128,256]{1,0:T(8,128)}) %all-reduce.5.cloned.1.call-update) | async-done | bytes 131088 | tf_op jit(solution)/shard_map/psum | solution.py:86
  249.1 3.6 %fusion.6 = f32[1536,256]{0,1:T(8,128)} fusion(f32[1536,128]{1,0:T(8,128)S(1)} %copy-done, f32[128,256]{1,0:T(8,128)} %all-reduce.5.cloned.1.call-done, f32[128]{0:T(128)S(1)} %copy-done.6), kind=kOutput, calls=%fused_computation.15 | convolution fusion | flops 604405760 | bytes 2490880 | tf_op jit(solution)/shard_map/dot_general | solution.py:87
  252.7 1.9 copy.10
  254.6 8.9 %scatter_fusion = f32[128,256]{1,0:T(8,128)S(1)} fusion(f32[128,256]{1,0:T(8,128)S(1)} %fusion.28, s32[1536]{0:T(1024)S(1)} %compare_select_fusion.1, f32[1536,256]{1,0:T(8,128)S(1)} %copy.10), kind=kCustom, calls=%fused_computation.3 | custom fusion | flops 393216 | bytes 4724736 | tf_op jit(solution)/shard_map/scatter-add | solution.py:88
  263.5 0.7 multiply_subtract_fusion
  (73 shorter events, 5.3 us)
Async XLA Ops:
  7.2 115.9 %copy-start = (f32[1536,128]{1,0:T(8,128)S(1)}, f32[1536,128]{1,0:T(8,128)}, u32[]{:S(2)}) copy-start(f32[1536,128]{1,0:T(8,128)} %param.16) | copy-start | bytes 2359300
  7.2 5.6 %copy-start.3 = (bf16[128,768]{1,0:T(8,128)(2,1)S(1)}, bf16[128,768]{1,0:T(8,128)(2,1)}, u32[]{:S(2)}) copy-start(bf16[128,768]{1,0:T(8,128)(2,1)} %param.13) | copy-start | bytes 589828
  7.2 101.1 %all-reduce.3.cloned.1.call-start = ((), (), s32[]{:S(2)}) async-start(), calls=%async_computation | async-start | bytes 262144 | tf_op jit(solution)/shard_map/psum | solution.py:69
  12.8 53.7 %copy-start.5 = (s32[1536]{0:T(1024)S(1)}, s32[1536]{0:T(1024)}, u32[]{:S(2)}) copy-start(s32[1536]{0:T(1024)} %param.15) | copy-start | bytes 18436
  12.9 8.2 %collective-permute-start = (bf16[128,768]{1,0:T(8,128)(2,1)S(1)}, bf16[128,768]{1,0:T(8,128)(2,1)S(1)}, u32[]{:S(2)}, u32[]{:S(2)}) collective-permute-start(bf16[128,768]{1,0:T(8,128)(2,1)S(1)} %copy.17), channel_id=1, source_target_pairs={{28,0},{0,4},{4,8},{8,12},{12,16},{16,20},{20,24},{24,28},{29,1},{... | collective-permute-start | bytes 589832 | tf_op jit(solution)/shard_map/while/body/eval_jaxpr/ppermute | solution.py:14
  14.0 7.1 %collective-permute-start.1 = (f32[128,256]{1,0:T(8,128)S(1)}, f32[128,256]{1,0:T(8,128)S(1)}, u32[]{:S(2)}, u32[]{:S(2)}) collective-permute-start(f32[128,256]{1,0:T(8,128)S(1)} %convolution_add_fusion.3), channel_id=1, source_target_pairs={{28,0},{0,4},{4,8},{8,12},{12,16},{16,20},{20,24},{24,28},{29,1},{... | collective-permute-start | bytes 393224 | tf_op jit(solution)/shard_map/while/body/eval_jaxpr/ppermute | solution.py:14
  21.1 7.5 %collective-permute-start = (bf16[128,768]{1,0:T(8,128)(2,1)S(1)}, bf16[128,768]{1,0:T(8,128)(2,1)S(1)}, u32[]{:S(2)}, u32[]{:S(2)}) collective-permute-start(bf16[128,768]{1,0:T(8,128)(2,1)S(1)} %copy.17), channel_id=1, source_target_pairs={{28,0},{0,4},{4,8},{8,12},{12,16},{16,20},{20,24},{24,28},{29,1},{... | collective-permute-start | bytes 589832 | tf_op jit(solution)/shard_map/while/body/eval_jaxpr/ppermute | solution.py:14
  21.7 6.8 %collective-permute-start.1 = (f32[128,256]{1,0:T(8,128)S(1)}, f32[128,256]{1,0:T(8,128)S(1)}, u32[]{:S(2)}, u32[]{:S(2)}) collective-permute-start(f32[128,256]{1,0:T(8,128)S(1)} %convolution_add_fusion.3), channel_id=1, source_target_pairs={{28,0},{0,4},{4,8},{8,12},{12,16},{16,20},{20,24},{24,28},{29,1},{... | collective-permute-start | bytes 393224 | tf_op jit(solution)/shard_map/while/body/eval_jaxpr/ppermute | solution.py:14
  28.5 7.5 %collective-permute-start = (bf16[128,768]{1,0:T(8,128)(2,1)S(1)}, bf16[128,768]{1,0:T(8,128)(2,1)S(1)}, u32[]{:S(2)}, u32[]{:S(2)}) collective-permute-start(bf16[128,768]{1,0:T(8,128)(2,1)S(1)} %copy.17), channel_id=1, source_target_pairs={{28,0},{0,4},{4,8},{8,12},{12,16},{16,20},{20,24},{24,28},{29,1},{... | collective-permute-start | bytes 589832 | tf_op jit(solution)/shard_map/while/body/eval_jaxpr/ppermute | solution.py:14
  29.2 6.8 %collective-permute-start.1 = (f32[128,256]{1,0:T(8,128)S(1)}, f32[128,256]{1,0:T(8,128)S(1)}, u32[]{:S(2)}, u32[]{:S(2)}) collective-permute-start(f32[128,256]{1,0:T(8,128)S(1)} %convolution_add_fusion.3), channel_id=1, source_target_pairs={{28,0},{0,4},{4,8},{8,12},{12,16},{16,20},{20,24},{24,28},{29,1},{... | collective-permute-start | bytes 393224 | tf_op jit(solution)/shard_map/while/body/eval_jaxpr/ppermute | solution.py:14
  36.0 7.5 %collective-permute-start = (bf16[128,768]{1,0:T(8,128)(2,1)S(1)}, bf16[128,768]{1,0:T(8,128)(2,1)S(1)}, u32[]{:S(2)}, u32[]{:S(2)}) collective-permute-start(bf16[128,768]{1,0:T(8,128)(2,1)S(1)} %copy.17), channel_id=1, source_target_pairs={{28,0},{0,4},{4,8},{8,12},{12,16},{16,20},{20,24},{24,28},{29,1},{... | collective-permute-start | bytes 589832 | tf_op jit(solution)/shard_map/while/body/eval_jaxpr/ppermute | solution.py:14
  36.6 6.8 %collective-permute-start.1 = (f32[128,256]{1,0:T(8,128)S(1)}, f32[128,256]{1,0:T(8,128)S(1)}, u32[]{:S(2)}, u32[]{:S(2)}) collective-permute-start(f32[128,256]{1,0:T(8,128)S(1)} %convolution_add_fusion.3), channel_id=1, source_target_pairs={{28,0},{0,4},{4,8},{8,12},{12,16},{16,20},{20,24},{24,28},{29,1},{... | collective-permute-start | bytes 393224 | tf_op jit(solution)/shard_map/while/body/eval_jaxpr/ppermute | solution.py:14
  43.5 7.5 %collective-permute-start = (bf16[128,768]{1,0:T(8,128)(2,1)S(1)}, bf16[128,768]{1,0:T(8,128)(2,1)S(1)}, u32[]{:S(2)}, u32[]{:S(2)}) collective-permute-start(bf16[128,768]{1,0:T(8,128)(2,1)S(1)} %copy.17), channel_id=1, source_target_pairs={{28,0},{0,4},{4,8},{8,12},{12,16},{16,20},{20,24},{24,28},{29,1},{... | collective-permute-start | bytes 589832 | tf_op jit(solution)/shard_map/while/body/eval_jaxpr/ppermute | solution.py:14
  44.1 6.8 %collective-permute-start.1 = (f32[128,256]{1,0:T(8,128)S(1)}, f32[128,256]{1,0:T(8,128)S(1)}, u32[]{:S(2)}, u32[]{:S(2)}) collective-permute-start(f32[128,256]{1,0:T(8,128)S(1)} %convolution_add_fusion.3), channel_id=1, source_target_pairs={{28,0},{0,4},{4,8},{8,12},{12,16},{16,20},{20,24},{24,28},{29,1},{... | collective-permute-start | bytes 393224 | tf_op jit(solution)/shard_map/while/body/eval_jaxpr/ppermute | solution.py:14
  51.0 7.5 %collective-permute-start = (bf16[128,768]{1,0:T(8,128)(2,1)S(1)}, bf16[128,768]{1,0:T(8,128)(2,1)S(1)}, u32[]{:S(2)}, u32[]{:S(2)}) collective-permute-start(bf16[128,768]{1,0:T(8,128)(2,1)S(1)} %copy.17), channel_id=1, source_target_pairs={{28,0},{0,4},{4,8},{8,12},{12,16},{16,20},{20,24},{24,28},{29,1},{... | collective-permute-start | bytes 589832 | tf_op jit(solution)/shard_map/while/body/eval_jaxpr/ppermute | solution.py:14
  51.6 6.8 %collective-permute-start.1 = (f32[128,256]{1,0:T(8,128)S(1)}, f32[128,256]{1,0:T(8,128)S(1)}, u32[]{:S(2)}, u32[]{:S(2)}) collective-permute-start(f32[128,256]{1,0:T(8,128)S(1)} %convolution_add_fusion.3), channel_id=1, source_target_pairs={{28,0},{0,4},{4,8},{8,12},{12,16},{16,20},{20,24},{24,28},{29,1},{... | collective-permute-start | bytes 393224 | tf_op jit(solution)/shard_map/while/body/eval_jaxpr/ppermute | solution.py:14
  58.4 7.5 %collective-permute-start = (bf16[128,768]{1,0:T(8,128)(2,1)S(1)}, bf16[128,768]{1,0:T(8,128)(2,1)S(1)}, u32[]{:S(2)}, u32[]{:S(2)}) collective-permute-start(bf16[128,768]{1,0:T(8,128)(2,1)S(1)} %copy.17), channel_id=1, source_target_pairs={{28,0},{0,4},{4,8},{8,12},{12,16},{16,20},{20,24},{24,28},{29,1},{... | collective-permute-start | bytes 589832 | tf_op jit(solution)/shard_map/while/body/eval_jaxpr/ppermute | solution.py:14
  59.1 6.8 %collective-permute-start.1 = (f32[128,256]{1,0:T(8,128)S(1)}, f32[128,256]{1,0:T(8,128)S(1)}, u32[]{:S(2)}, u32[]{:S(2)}) collective-permute-start(f32[128,256]{1,0:T(8,128)S(1)} %convolution_add_fusion.3), channel_id=1, source_target_pairs={{28,0},{0,4},{4,8},{8,12},{12,16},{16,20},{20,24},{24,28},{29,1},{... | collective-permute-start | bytes 393224 | tf_op jit(solution)/shard_map/while/body/eval_jaxpr/ppermute | solution.py:14
  65.9 6.6 %copy-start.1 = (f32[256,256]{1,0:T(8,128)S(1)}, f32[256,256]{1,0:T(8,128)}, u32[]{:S(2)}) copy-start(f32[256,256]{1,0:T(8,128)} %param.11) | copy-start | bytes 786436
  66.4 5.3 %collective-permute-start.2 = (f32[128,256]{1,0:T(8,128)S(1)}, f32[128,256]{1,0:T(8,128)S(1)}, u32[]{:S(2)}, u32[]{:S(2)}) collective-permute-start(f32[128,256]{1,0:T(8,128)S(1)} %convolution_add_fusion.1), channel_id=1, source_target_pairs={{28,0},{0,4},{4,8},{8,12},{12,16},{16,20},{20,24},{24,28},{29,1},{... | collective-permute-start | bytes 393224 | tf_op jit(solution)/shard_map/ppermute | solution.py:14
  71.8 0.7 copy-start.4
  72.4 176.6 %all-reduce.5.cloned.1.call-start = ((), (), s32[]{:S(2)}) async-start(), calls=%async_computation.1 | async-start | bytes 262144 | tf_op jit(solution)/shard_map/psum | solution.py:86
  123.1 126.0 %copy-start.6 = (f32[128]{0:T(128)S(1)}, f32[128]{0:T(128)}, u32[]{:S(2)}) copy-start(f32[128]{0:T(128)} %param.17) | copy-start | bytes 1540
  254.6 8.9 %copy-start.2 = (f32[128,256]{1,0:T(8,128)S(1)}, f32[128,256]{1,0:T(8,128)}, u32[]{:S(2)}) copy-start(f32[128,256]{1,0:T(8,128)} %param.14) | copy-start | bytes 393220
Sparse Core Ops, SparseCore 0:
  72.6 35.7 all-reduce.2
  125.8 123.2 all-reduce.4
where the time goes:
time: 271 us
  waiting for transfers between devices  206 us (76%)
  other arithmetic  15 us (6%)
  between operations  14.3 us (5%)
  blocking collectives  9.79 us (4%)
  local copies, waits for them, and re-layouts  9.77 us (4%)
  matrix products  9.7 us (4%)
  starting transfers between devices  5.97 us (2%)
    psum x1, waiting for transfers between devices, local(): projected = lax.psum(local_proj, ('blk', 'col'))  123 us
    ppermute x15, waiting for transfers between devices, shifted(): return lax.ppermute(block, axis, route)  48.3 us
    psum x1, waiting for transfers between devices, local(): prediction = lax.psum(partial_value, 'col')  35 us
    all_gather x1, blocking collectives, local(): lax.all_gather(residual_full.astype(jnp.bfloat16), 'blk', axis=0, tiled=T...  9.79 us
    scatter-add x1, other arithmetic, local(): adjusted = gradient.at[position].add(-correction, mode='drop')  8.88 us
    ppermute x15, starting transfers between devices, shifted(): return lax.ppermute(block, axis, route)  5.89 us
  transfers between devices with their start and end apart: 17, of which 10 were waited for; matrix products, arithmetic and copies ran while one was open for 2% of the time, Pallas kernels for 0%

commit v1 on v0

--- a/solution.py
+++ b/solution.py
@@ -66,7 +66,8 @@
     )
     partial_value = pass_up(partial_value)
     share_rows = blk_rows // columns
-    prediction = lax.psum(partial_value, "col")
+    parts = lax.all_gather(partial_value, "col")
+    prediction = jnp.sum(parts, axis=0)
     residual_full = prediction - wanted
     gathered = lax.all_gather(residual_full.astype(jnp.bfloat16), "blk", axis=0, tiled=True)
     own_resid = lax.dynamic_slice_in_dim(

time: 271 us -> 251 us (0.926)
  waiting for transfers between devices: 206 us -> 171 us
  blocking collectives: 9.79 us -> 26.7 us
    psum x1 -> x0, waiting for transfers between devices: 35 us -> none  [local(): prediction = lax.psum(partial_value, 'col')]
    all_gather x0 -> x1, blocking collectives: none -> 16.9 us  [local(): parts = lax.all_gather(partial_value, 'col')]
  transfers between devices with their start and end apart: 17 -> 16, of which waited for: 10 -> 9; matrix products, arithmetic and copies ran while one was open for 2% -> 2% of each run, Pallas kernels for 0% -> 0%
where the time goes in v1:
time: 251 us
  waiting for transfers between devices  171 us (68%)
  blocking collectives  26.7 us (11%)
  between operations  14.2 us (6%)
  other arithmetic  14.1 us (6%)
  matrix products  9.68 us (4%)
  local copies, waits for them, and re-layouts  9.4 us (4%)
  starting transfers between devices  5.92 us (2%)
    psum x1, waiting for transfers between devices, local(): projected = lax.psum(local_proj, ('blk', 'col'))  123 us
    ppermute x15, waiting for transfers between devices, shifted(): return lax.ppermute(block, axis, route)  47.2 us
    all_gather x1, blocking collectives, local(): parts = lax.all_gather(partial_value, 'col')  16.9 us
    all_gather x1, blocking collectives, local(): lax.all_gather(residual_full.astype(jnp.bfloat16), 'blk', axis=0, tiled=T...  9.85 us
    scatter-add x1, other arithmetic, local(): adjusted = gradient.at[position].add(-correction, mode='drop')  8.88 us
    ppermute x15, starting transfers between devices, shifted(): return lax.ppermute(block, axis, route)  5.88 us
  transfers between devices with their start and end apart: 16, of which 9 were waited for; matrix products, arithmetic and copies ran while one was open for 2% of the time, Pallas kernels for 0%

profile of v1, /device:TPU:0, one launch (start us, length us, event | category | flops | bytes accessed | tf_op | source)
XLA Modules:
  0.0 251.2 jit_solution(10583542001570277191)
XLA Ops:
  7.2 0.8 compare_and_fusion.2
  8.0 0.7 compare_select_fusion.2
  8.7 1.0 multiply_reduce_fusion.2
  9.7 0.9 convert_element_type.36
  10.6 2.0 gather_fusion
  12.8 53.1 %while.19 = (s32[]{:T(128)}, bf16[128,768]{1,0:T(8,128)(2,1)S(1)}, f32[128,256]{1,0:T(8,128)S(1)}, bf16[1024,128]{1,0:T(8,128)(2,1)S(1)}, f32[128]{0:T(128)S(1)}...) while((s32[]{:T(128)}, bf16[128,768]{1,0:T(8,128)(2,1)S(1)}, ...), condition=%wide.region_3.4_spmd, body=%wide.region_1.3_spmd.sunk | while | flops 33980304 | bytes 2721664 | solution.py:63
  12.9 0.5 collective-permute-start
  14.0 2.6 %collective-permute-start.1 = (f32[128,256]{1,0:T(8,128)S(1)}, f32[128,256]{1,0:T(8,128)S(1)}, u32[]{:S(2)}, u32[]{:S(2)}) collective-permute-start(f32[128,256]{1,0:T(8,128)S(1)} %convolution_add_fusion.3), channel_id=1, source_target_pairs={{28,0},{0,4},{4,8},{8,12},{12,16},{16,20},{20,24},{24,28},{29,1},{... | collective-permute-start | bytes 393224 | tf_op jit(solution)/shard_map/while/body/eval_jaxpr/ppermute | solution.py:14
  16.6 4.4 %collective-permute-done.1 = f32[128,256]{1,0:T(8,128)S(1)} collective-permute-done((f32[128,256]{1,0:T(8,128)S(1)}, f32[128,256]{1,0:T(8,128)S(1)}, u32[]{:S(2)}, u32[]{:S(2)}) %collective-permute-start.1) | collective-permute-done | bytes 131104 | tf_op jit(solution)/shard_map/while/body/eval_jaxpr/ppermute | solution.py:14
  21.7 1.5 collective-permute-start.1
  23.2 5.3 %collective-permute-done.1 = f32[128,256]{1,0:T(8,128)S(1)} collective-permute-done((f32[128,256]{1,0:T(8,128)S(1)}, f32[128,256]{1,0:T(8,128)S(1)}, u32[]{:S(2)}, u32[]{:S(2)}) %collective-permute-start.1) | collective-permute-done | bytes 131104 | tf_op jit(solution)/shard_map/while/body/eval_jaxpr/ppermute | solution.py:14
  29.2 0.6 collective-permute-start.1
  29.7 6.2 %collective-permute-done.1 = f32[128,256]{1,0:T(8,128)S(1)} collective-permute-done((f32[128,256]{1,0:T(8,128)S(1)}, f32[128,256]{1,0:T(8,128)S(1)}, u32[]{:S(2)}, u32[]{:S(2)}) %collective-permute-start.1) | collective-permute-done | bytes 131104 | tf_op jit(solution)/shard_map/while/body/eval_jaxpr/ppermute | solution.py:14
  36.7 6.8 %collective-permute-done.1 = f32[128,256]{1,0:T(8,128)S(1)} collective-permute-done((f32[128,256]{1,0:T(8,128)S(1)}, f32[128,256]{1,0:T(8,128)S(1)}, u32[]{:S(2)}, u32[]{:S(2)}) %collective-permute-start.1) | collective-permute-done | bytes 131104 | tf_op jit(solution)/shard_map/while/body/eval_jaxpr/ppermute | solution.py:14
  43.7 0.3 constant_dynamic-update-slice_fusion.3
  44.2 6.8 %collective-permute-done.1 = f32[128,256]{1,0:T(8,128)S(1)} collective-permute-done((f32[128,256]{1,0:T(8,128)S(1)}, f32[128,256]{1,0:T(8,128)S(1)}, u32[]{:S(2)}, u32[]{:S(2)}) %collective-permute-start.1) | collective-permute-done | bytes 131104 | tf_op jit(solution)/shard_map/while/body/eval_jaxpr/ppermute | solution.py:14
  51.7 6.8 %collective-permute-done.1 = f32[128,256]{1,0:T(8,128)S(1)} collective-permute-done((f32[128,256]{1,0:T(8,128)S(1)}, f32[128,256]{1,0:T(8,128)S(1)}, u32[]{:S(2)}, u32[]{:S(2)}) %collective-permute-start.1) | collective-permute-done | bytes 131104 | tf_op jit(solution)/shard_map/while/body/eval_jaxpr/ppermute | solution.py:14
  59.1 6.8 %collective-permute-done.1 = f32[128,256]{1,0:T(8,128)S(1)} collective-permute-done((f32[128,256]{1,0:T(8,128)S(1)}, f32[128,256]{1,0:T(8,128)S(1)}, u32[]{:S(2)}, u32[]{:S(2)}) %collective-permute-start.1) | collective-permute-done | bytes 131104 | tf_op jit(solution)/shard_map/while/body/eval_jaxpr/ppermute | solution.py:14
  66.5 0.3 copy-done.1
  66.8 0.8 gather_fusion.1
  67.6 4.2 %collective-permute-done.2 = f32[128,256]{1,0:T(8,128)S(1)} collective-permute-done((f32[128,256]{1,0:T(8,128)S(1)}, f32[128,256]{1,0:T(8,128)S(1)}, u32[]{:S(2)}, u32[]{:S(2)}) %collective-permute-start.2) | collective-permute-done | bytes 131104 | tf_op jit(solution)/shard_map/ppermute | solution.py:14
  71.8 16.9 %all-gather = f32[512,256]{1,0:T(8,128)S(1)} all-gather(f32[128,256]{1,0:T(8,128)S(1)} %collective-permute-done.2), channel_id=2, replica_groups=mesh['blk'=8,'col'=4] {'col'}, dimensions={0}, use_global_device_ids=true | all-gather | bytes 655360 | tf_op jit(solution)/shard_map/all_gather | solution.py:69
  88.8 9.9 %all_gather.11 = bf16[1024,256]{1,0:T(8,128)(2,1)S(1)} all-gather(bf16[128,256]{1,0:T(8,128)(2,1)S(1)} %get-tuple-element.224), channel_id=1, replica_groups=mesh['blk'=8,'col'=4] {'blk'}, dimensions={0}, use_global_device_ids=true | all-gather | bytes 589824 | tf_op jit(solution)/shard_map/all_gather | solution.py:72
  98.6 0.3 fusion.28
  98.9 3.7 %gather_fusion.2 = f32[1536,256]{1,0:T(8,128)S(1)} fusion(f32[128,256]{1,0:T(8,128)S(1)} %fusion.28, s32[2048]{0:T(1024)S(1)} %pad_clamp_fusion), kind=kCustom, calls=%fused_computation.2 | custom fusion | bytes 3151872 | tf_op jit(solution)/shard_map/jit(_take)/gather | solution.py:84
  102.6 2.6 %fusion.10 = f32[128,256]{1,0:T(8,128)} fusion(f32[1536,128]{1,0:T(8,128)S(1)} %copy-done, f32[1536,256]{1,0:T(8,128)S(1)} %gather_fusion.2, pred[1536]{0:T(1024)(128)(4,1)S(1)} %get-tuple-element.222, pred[1536]{0:T(1024)(128)(4,1)S(1)} %get-tuple-element.228), kind=kOutput, calls=%fused_computation.19 | convolution fusion | flops 604766208 | bytes 2493440 | tf_op jit(solution)/shard_map/dot_general | solution.py:86
  105.2 0.6 constant_dynamic-slice_fusion
  105.8 123.5 %all-reduce.2.cloned.1.call-done = f32[128,256]{1,0:T(8,128)} async-done(((f32[128,256]{1,0:T(8,128)}), f32[128,256]{1,0:T(8,128)}) %all-reduce.2.cloned.1.call-update) | async-done | bytes 131088 | tf_op jit(solution)/shard_map/psum | solution.py:87
  229.3 3.6 %fusion.6 = f32[1536,256]{0,1:T(8,128)} fusion(f32[1536,128]{1,0:T(8,128)S(1)} %copy-done, f32[128,256]{1,0:T(8,128)} %all-reduce.2.cloned.1.call-done, f32[128]{0:T(128)S(1)} %copy-done.5), kind=kOutput, calls=%fused_computation.15 | convolution fusion | flops 604405760 | bytes 2490880 | tf_op jit(solution)/shard_map/dot_general | solution.py:88
  232.8 1.9 copy.10
  234.7 8.9 %scatter_fusion = f32[128,256]{1,0:T(8,128)S(1)} fusion(f32[128,256]{1,0:T(8,128)S(1)} %fusion.28, s32[1536]{0:T(1024)S(1)} %compare_select_fusion.1, f32[1536,256]{1,0:T(8,128)S(1)} %copy.10), kind=kCustom, calls=%fused_computation.3 | custom fusion | flops 393216 | bytes 4724736 | tf_op jit(solution)/shard_map/scatter-add | solution.py:89
  243.6 0.7 multiply_subtract_fusion
  (70 shorter events, 5.1 us)
Async XLA Ops:
  7.2 95.4 %copy-start = (f32[1536,128]{1,0:T(8,128)S(1)}, f32[1536,128]{1,0:T(8,128)}, u32[]{:S(2)}) copy-start(f32[1536,128]{1,0:T(8,128)} %param.16) | copy-start | bytes 2359300
  7.2 5.6 %copy-start.3 = (bf16[128,768]{1,0:T(8,128)(2,1)S(1)}, bf16[128,768]{1,0:T(8,128)(2,1)}, u32[]{:S(2)}) copy-start(bf16[128,768]{1,0:T(8,128)(2,1)} %param.13) | copy-start | bytes 589828
  7.2 222.1 %all-reduce.2.cloned.1.call-start = ((), (), s32[]{:S(2)}) async-start(), calls=%async_computation | async-start | bytes 262144 | tf_op jit(solution)/shard_map/psum | solution.py:87
  12.8 53.7 %copy-start.4 = (s32[1536]{0:T(1024)S(1)}, s32[1536]{0:T(1024)}, u32[]{:S(2)}) copy-start(s32[1536]{0:T(1024)} %param.15) | copy-start | bytes 18436
  12.9 8.2 %collective-permute-start = (bf16[128,768]{1,0:T(8,128)(2,1)S(1)}, bf16[128,768]{1,0:T(8,128)(2,1)S(1)}, u32[]{:S(2)}, u32[]{:S(2)}) collective-permute-start(bf16[128,768]{1,0:T(8,128)(2,1)S(1)} %copy.17), channel_id=1, source_target_pairs={{28,0},{0,4},{4,8},{8,12},{12,16},{16,20},{20,24},{24,28},{29,1},{... | collective-permute-start | bytes 589832 | tf_op jit(solution)/shard_map/while/body/eval_jaxpr/ppermute | solution.py:14
  14.0 7.1 %collective-permute-start.1 = (f32[128,256]{1,0:T(8,128)S(1)}, f32[128,256]{1,0:T(8,128)S(1)}, u32[]{:S(2)}, u32[]{:S(2)}) collective-permute-start(f32[128,256]{1,0:T(8,128)S(1)} %convolution_add_fusion.3), channel_id=1, source_target_pairs={{28,0},{0,4},{4,8},{8,12},{12,16},{16,20},{20,24},{24,28},{29,1},{... | collective-permute-start | bytes 393224 | tf_op jit(solution)/shard_map/while/body/eval_jaxpr/ppermute | solution.py:14
  21.1 7.5 %collective-permute-start = (bf16[128,768]{1,0:T(8,128)(2,1)S(1)}, bf16[128,768]{1,0:T(8,128)(2,1)S(1)}, u32[]{:S(2)}, u32[]{:S(2)}) collective-permute-start(bf16[128,768]{1,0:T(8,128)(2,1)S(1)} %copy.17), channel_id=1, source_target_pairs={{28,0},{0,4},{4,8},{8,12},{12,16},{16,20},{20,24},{24,28},{29,1},{... | collective-permute-start | bytes 589832 | tf_op jit(solution)/shard_map/while/body/eval_jaxpr/ppermute | solution.py:14
  21.7 6.8 %collective-permute-start.1 = (f32[128,256]{1,0:T(8,128)S(1)}, f32[128,256]{1,0:T(8,128)S(1)}, u32[]{:S(2)}, u32[]{:S(2)}) collective-permute-start(f32[128,256]{1,0:T(8,128)S(1)} %convolution_add_fusion.3), channel_id=1, source_target_pairs={{28,0},{0,4},{4,8},{8,12},{12,16},{16,20},{20,24},{24,28},{29,1},{... | collective-permute-start | bytes 393224 | tf_op jit(solution)/shard_map/while/body/eval_jaxpr/ppermute | solution.py:14
  28.5 7.5 %collective-permute-start = (bf16[128,768]{1,0:T(8,128)(2,1)S(1)}, bf16[128,768]{1,0:T(8,128)(2,1)S(1)}, u32[]{:S(2)}, u32[]{:S(2)}) collective-permute-start(bf16[128,768]{1,0:T(8,128)(2,1)S(1)} %copy.17), channel_id=1, source_target_pairs={{28,0},{0,4},{4,8},{8,12},{12,16},{16,20},{20,24},{24,28},{29,1},{... | collective-permute-start | bytes 589832 | tf_op jit(solution)/shard_map/while/body/eval_jaxpr/ppermute | solution.py:14
  29.2 6.8 %collective-permute-start.1 = (f32[128,256]{1,0:T(8,128)S(1)}, f32[128,256]{1,0:T(8,128)S(1)}, u32[]{:S(2)}, u32[]{:S(2)}) collective-permute-start(f32[128,256]{1,0:T(8,128)S(1)} %convolution_add_fusion.3), channel_id=1, source_target_pairs={{28,0},{0,4},{4,8},{8,12},{12,16},{16,20},{20,24},{24,28},{29,1},{... | collective-permute-start | bytes 393224 | tf_op jit(solution)/shard_map/while/body/eval_jaxpr/ppermute | solution.py:14
  36.0 7.5 %collective-permute-start = (bf16[128,768]{1,0:T(8,128)(2,1)S(1)}, bf16[128,768]{1,0:T(8,128)(2,1)S(1)}, u32[]{:S(2)}, u32[]{:S(2)}) collective-permute-start(bf16[128,768]{1,0:T(8,128)(2,1)S(1)} %copy.17), channel_id=1, source_target_pairs={{28,0},{0,4},{4,8},{8,12},{12,16},{16,20},{20,24},{24,28},{29,1},{... | collective-permute-start | bytes 589832 | tf_op jit(solution)/shard_map/while/body/eval_jaxpr/ppermute | solution.py:14
  36.6 6.8 %collective-permute-start.1 = (f32[128,256]{1,0:T(8,128)S(1)}, f32[128,256]{1,0:T(8,128)S(1)}, u32[]{:S(2)}, u32[]{:S(2)}) collective-permute-start(f32[128,256]{1,0:T(8,128)S(1)} %convolution_add_fusion.3), channel_id=1, source_target_pairs={{28,0},{0,4},{4,8},{8,12},{12,16},{16,20},{20,24},{24,28},{29,1},{... | collective-permute-start | bytes 393224 | tf_op jit(solution)/shard_map/while/body/eval_jaxpr/ppermute | solution.py:14
  43.5 7.5 %collective-permute-start = (bf16[128,768]{1,0:T(8,128)(2,1)S(1)}, bf16[128,768]{1,0:T(8,128)(2,1)S(1)}, u32[]{:S(2)}, u32[]{:S(2)}) collective-permute-start(bf16[128,768]{1,0:T(8,128)(2,1)S(1)} %copy.17), channel_id=1, source_target_pairs={{28,0},{0,4},{4,8},{8,12},{12,16},{16,20},{20,24},{24,28},{29,1},{... | collective-permute-start | bytes 589832 | tf_op jit(solution)/shard_map/while/body/eval_jaxpr/ppermute | solution.py:14
  44.1 6.8 %collective-permute-start.1 = (f32[128,256]{1,0:T(8,128)S(1)}, f32[128,256]{1,0:T(8,128)S(1)}, u32[]{:S(2)}, u32[]{:S(2)}) collective-permute-start(f32[128,256]{1,0:T(8,128)S(1)} %convolution_add_fusion.3), channel_id=1, source_target_pairs={{28,0},{0,4},{4,8},{8,12},{12,16},{16,20},{20,24},{24,28},{29,1},{... | collective-permute-start | bytes 393224 | tf_op jit(solution)/shard_map/while/body/eval_jaxpr/ppermute | solution.py:14
  51.0 7.5 %collective-permute-start = (bf16[128,768]{1,0:T(8,128)(2,1)S(1)}, bf16[128,768]{1,0:T(8,128)(2,1)S(1)}, u32[]{:S(2)}, u32[]{:S(2)}) collective-permute-start(bf16[128,768]{1,0:T(8,128)(2,1)S(1)} %copy.17), channel_id=1, source_target_pairs={{28,0},{0,4},{4,8},{8,12},{12,16},{16,20},{20,24},{24,28},{29,1},{... | collective-permute-start | bytes 589832 | tf_op jit(solution)/shard_map/while/body/eval_jaxpr/ppermute | solution.py:14
  51.6 6.8 %collective-permute-start.1 = (f32[128,256]{1,0:T(8,128)S(1)}, f32[128,256]{1,0:T(8,128)S(1)}, u32[]{:S(2)}, u32[]{:S(2)}) collective-permute-start(f32[128,256]{1,0:T(8,128)S(1)} %convolution_add_fusion.3), channel_id=1, source_target_pairs={{28,0},{0,4},{4,8},{8,12},{12,16},{16,20},{20,24},{24,28},{29,1},{... | collective-permute-start | bytes 393224 | tf_op jit(solution)/shard_map/while/body/eval_jaxpr/ppermute | solution.py:14
  58.4 7.5 %collective-permute-start = (bf16[128,768]{1,0:T(8,128)(2,1)S(1)}, bf16[128,768]{1,0:T(8,128)(2,1)S(1)}, u32[]{:S(2)}, u32[]{:S(2)}) collective-permute-start(bf16[128,768]{1,0:T(8,128)(2,1)S(1)} %copy.17), channel_id=1, source_target_pairs={{28,0},{0,4},{4,8},{8,12},{12,16},{16,20},{20,24},{24,28},{29,1},{... | collective-permute-start | bytes 589832 | tf_op jit(solution)/shard_map/while/body/eval_jaxpr/ppermute | solution.py:14
  59.1 6.8 %collective-permute-start.1 = (f32[128,256]{1,0:T(8,128)S(1)}, f32[128,256]{1,0:T(8,128)S(1)}, u32[]{:S(2)}, u32[]{:S(2)}) collective-permute-start(f32[128,256]{1,0:T(8,128)S(1)} %convolution_add_fusion.3), channel_id=1, source_target_pairs={{28,0},{0,4},{4,8},{8,12},{12,16},{16,20},{20,24},{24,28},{29,1},{... | collective-permute-start | bytes 393224 | tf_op jit(solution)/shard_map/while/body/eval_jaxpr/ppermute | solution.py:14
  65.9 1.0 copy-start.1
  66.4 5.3 %collective-permute-start.2 = (f32[128,256]{1,0:T(8,128)S(1)}, f32[128,256]{1,0:T(8,128)S(1)}, u32[]{:S(2)}, u32[]{:S(2)}) collective-permute-start(f32[128,256]{1,0:T(8,128)S(1)} %convolution_add_fusion.1), channel_id=1, source_target_pairs={{28,0},{0,4},{4,8},{8,12},{12,16},{16,20},{20,24},{24,28},{29,1},{... | collective-permute-start | bytes 393224 | tf_op jit(solution)/shard_map/ppermute | solution.py:14
  102.6 126.7 %copy-start.5 = (f32[128]{0:T(128)S(1)}, f32[128]{0:T(128)}, u32[]{:S(2)}) copy-start(f32[128]{0:T(128)} %param.17) | copy-start | bytes 1540
  234.7 8.9 %copy-start.2 = (f32[128,256]{1,0:T(8,128)S(1)}, f32[128,256]{1,0:T(8,128)}, u32[]{:S(2)}) copy-start(f32[128,256]{1,0:T(8,128)} %param.14) | copy-start | bytes 393220
Sparse Core Ops, SparseCore 0:
  105.3 123.9 all-reduce.1
